TPU v7x, 256 devices: a 4x2x16 block of a 4x16x16 slice. The times are simulated.
256 devices in a mesh: groups: 2 (over y), ep: 128 (over x, z, core).
Axes of the slice: x: 4, y: 2, z: 16, core: 2. Of those that a mesh axis runs over, the one named last changes fastest.
The devices are a block of a 4x16x16 slice.
Arguments:
- tokens: bfloat16 [4096, 2880], P(('groups', 'ep')), parts along dimension 0, may hold values from -6 to 6
- routes: int32 [4096, 4], P(('groups', 'ep')), parts along dimension 0, may hold values from 0 to 63, all different within a row; in each aligned block of 16 rows (0 to 15, 16 to 31, ...) at most 2 rows name the same one
- gate_fixed: int32 [4096, 4], P(('groups', 'ep')), parts along dimension 0, may hold values from 1 to 65535
- gate_weight: bfloat16 [128, 2880, 720], P('ep'), may hold values from -0.109375 to 0.109375
- up_weight: bfloat16 [128, 2880, 720], P('ep'), may hold values from -0.109375 to 0.109375
- down_weight: bfloat16 [128, 720, 2880], P('ep'), may hold values from -0.15625 to 0.15625
Outputs:
- mixed: bfloat16 [4096, 2880], P(('groups', 'ep')), parts along dimension 0
There are 2 independent parts, one for each index of `groups`. A program takes and returns all parts, laid end to end along the dimension named above; an argument that names none is the same for every part. Nothing has to cross between parts.
Inputs may be any that keep to these rules, and one draw needn't show every extreme that they name: `routes`: each row names 4 different experts; the 16 rows of one device name any one expert at most 2 times.
All inputs are finite; a program needn't handle non-finite values.
Results may differ from a plain program's by a relative error of at most 0.0065.
Values may be sent and summed in bfloat16 or wider, within the bound.
A program may use at most 64 MiB of HBM per device.

v0:
```python
import jax
import jax.numpy as jnp
from jax import lax
from jax.sharding import PartitionSpec as P


def swapped(value, axis, bit):
    mask = 2**bit
    pairs = [(source, source ^ mask) for source in range(lax.axis_size(axis))]
    return lax.ppermute(value, axis, pairs)


def expert_half(expert_rows, w_gate, w_up, w_down):
    gate_part = jnp.dot(expert_rows, w_gate, preferred_element_type=jnp.float32)
    up_part = jnp.dot(expert_rows, w_up, preferred_element_type=jnp.float32)
    hidden = (jax.nn.silu(gate_part) * up_part).astype(jnp.bfloat16)
    return jnp.dot(hidden, w_down, preferred_element_type=jnp.float32).astype(jnp.bfloat16)


def local(tokens, routes, gate_fixed, gate_weight, up_weight, down_weight):
    devices_ep = lax.axis_size("ep")
    experts = devices_ep // 2
    tok_count = tokens.shape[0]
    top_count = routes.shape[1]
    width = tokens.shape[1]
    capacity = 2 * tok_count * top_count // experts
    onehot = (routes[:, :, None] == jnp.arange(experts, dtype=jnp.int32)).astype(jnp.int32)
    flat_hot = onehot.reshape(tok_count * top_count, experts)
    before = jnp.cumsum(flat_hot, axis=0) - flat_hot
    position = jnp.sum(before * flat_hot, axis=1).reshape(tok_count, top_count)
    slot_index = routes * capacity + position
    select = (slot_index[:, :, None] == jnp.arange(experts * capacity, dtype=jnp.int32)).astype(
        jnp.int32
    )
    select = jnp.sum(select, axis=1).astype(jnp.bfloat16)
    packed = jnp.einsum("ts,td->sd", select, tokens, preferred_element_type=jnp.float32).astype(
        jnp.bfloat16
    )
    packed = packed.reshape(experts, 1, capacity, width)
    outgoing = jnp.broadcast_to(packed, (experts, 2, capacity, width)).reshape(
        devices_ep, capacity, width
    )
    received = lax.all_to_all(outgoing, "ep", split_axis=0, concat_axis=0, tiled=True)
    result = expert_half(received.reshape(-1, width), gate_weight[0], up_weight[0], down_weight[0])
    partial_value = result.reshape(received.shape[0], received.shape[1], width)
    parity = lax.axis_index("ep") % 2
    halves = partial_value.reshape(devices_ep, capacity, 2, width // 2)
    kept_half = lax.dynamic_index_in_dim(halves, parity, 2, keepdims=False)
    given_half = lax.dynamic_index_in_dim(halves, 1 - parity, 2, keepdims=False)
    partner = swapped(given_half, "ep", 0)
    reduced = (kept_half.astype(jnp.float32) + partner.astype(jnp.float32)).astype(jnp.bfloat16)
    returned = lax.all_to_all(reduced, "ep", split_axis=0, concat_axis=0, tiled=True)
    ordered = returned.reshape(experts, 2, capacity, width // 2).transpose(0, 2, 1, 3)
    expert_out = ordered.reshape(experts * capacity, width)
    picked = jnp.take(expert_out, slot_index.reshape(-1), axis=0).reshape(
        tok_count, top_count, width
    )
    weights = gate_fixed.astype(jnp.float32) / 65536.0
    mixed = jnp.sum(weights[:, :, None] * picked.astype(jnp.float32), axis=1)
    return mixed.astype(jnp.bfloat16)


def solution(mesh):
    placed = (
        P(("groups", "ep"), None),
        P(("groups", "ep"), None),
        P(("groups", "ep"), None),
        P("ep", None, None),
        P("ep", None, None),
        P("ep", None, None),
    )
    return jax.shard_map(
        local, mesh=mesh, in_specs=placed, out_specs=P(("groups", "ep"), None), check_vma=False
    )
```

profile of v0, /device:TPU:40, one launch (start us, length us, event | category | flops | bytes accessed | tf_op | source)
XLA Modules:
  0.0 197.8 jit_solution(10803944687454826425)
XLA Ops:
  0.0 0.8 copy.55
  0.8 0.1 eq.31
  1.0 0.1 reduce_window_sum.11
  1.1 0.2 select_reduce_fusion
  1.4 0.1 copy.57
  1.5 0.4 convolution_convert_fusion
  1.9 0.4 copy.58
  2.3 0.3 broadcast_in_dim.23
  2.6 1.9 broadcast_in_dim.24
  4.5 32.3 %all-to-all-start = ((bf16[128,2,2880]{2,1,0:T(2,128)(2,1)}), bf16[128,2,2880]{2,1,0:T(2,128)(2,1)S(1)}, u32[]{:S(2)}, u32[]{:S(2)}) async-start(bf16[128,2,2880]{2,1,0:T(2,128)(2,1)} %bitcast), calls=%async_computation | async-start | bytes 3014656 | tf_op jit(solution)/shard_map/all_to_all | solution.py:43
  36.9 71.7 %all-to-all-done = bf16[128,2,2880]{2,1,0:T(2,128)(2,1)S(1)} async-done(((bf16[128,2,2880]{2,1,0:T(2,128)(2,1)}), bf16[128,2,2880]{2,1,0:T(2,128)(2,1)S(1)}, u32[]{:S(2)}, u32[]{:S(2)}) %all-to-all-start) | async-done | bytes 1474592 | tf_op jit(solution)/shard_map/all_to_all | solution.py:43
  108.6 1.2 reshape.70
  109.8 3.5 %fusion.4 = f32[256,720]{0,1:T(8,128)S(1)} fusion(bf16[256,2880]{1,0:T(8,128)(2,1)S(1)} %reshape.70, bf16[1,2880,720]{1,2,0:T(8,128)(2,1)} %param.9), kind=kOutput, calls=%fused_computation.5 | convolution fusion | flops 1061683200 | bytes 6359040 | tf_op jit(solution)/shard_map/dot_general | solution.py:14
  113.3 9.4 %fusion.6 = bf16[256,2880]{0,1:T(8,128)(2,1)} fusion(bf16[1,720,2880]{2,1,0:T(8,128)(2,1)} %param.11, bf16[256,2880]{1,0:T(8,128)(2,1)S(1)} %reshape.70, bf16[1,2880,720]{1,2,0:T(8,128)(2,1)} %param.10, f32[256,720]{0,1:T(8,128)S(1)} %fusion.4), kind=kOutput, calls=%fused_computation.7 | convolution fusion | flops 2125209600 | bytes 11980800 | tf_op jit(solution)/shard_map/dot_general | solution.py:17
  122.7 1.8 copy.59
  124.6 1.9 reshape_reshape.3
  126.5 4.4 %constant_dynamic-slice_fusion.1 = (bf16[128,2,1,1440]{3,2,1,0:T(2,128)(2,1)S(1)}, bf16[128,2,1,1440]{3,2,1,0:T(2,128)(2,1)}) fusion(bf16[128,2,2,1440]{3,2,1,0:T(2,128)(2,1)S(1)} %reshape_reshape.3, s32[]{:T(128)S(6)} %select_n.38, s32[]{:T(128)S(6)} %select_n.39), kind=kLoop, calls=%fused_computation.28 | loop fusion | bytes 2949128 | tf_op jit(solution)/shard_map/jit(dynamic_index_in_dim)/dynamic_slice | solution.py:48
  130.9 4.1 %copy.61 = bf16[128,2,1,1440]{0,3,2,1:T(8,128)(2,1)S(1)} copy(bf16[128,2,1,1440]{3,2,1,0:T(2,128)(2,1)} %get-tuple-element.8) | data formatting | bytes 1474560 | tf_op jit(solution)/shard_map/jit(dynamic_index_in_dim)/dynamic_slice | solution.py:49
  135.0 0.1 collective-permute-start
  135.1 1.9 copy.64
  137.0 0.4 collective-permute-done
  137.4 1.4 fusion.9
  138.8 2.0 %copy.62 = bf16[128,2,1440]{2,1,0:T(2,128)(2,1)} copy(bf16[128,2,1440]{0,2,1:T(8,128)(2,1)S(1)} %fusion.9) | data formatting | bytes 1474560 | tf_op jit(solution)/shard_map/convert_element_type | solution.py:51
  140.8 11.8 %all-to-all-start.1 = ((bf16[128,2,1440]{2,1,0:T(2,128)(2,1)}), bf16[128,2,1440]{2,1,0:T(2,128)(2,1)S(1)}, u32[]{:S(2)}, u32[]{:S(2)}) async-start(bf16[128,2,1440]{2,1,0:T(2,128)(2,1)} %copy.62), calls=%async_computation.1 | async-start | bytes 1572864 | tf_op jit(solution)/shard_map/all_to_all | solution.py:52
  152.6 0.1 reshape.73
  152.8 0.1 copy.54
  152.8 41.6 %all-to-all-done.1 = bf16[128,2,1440]{2,1,0:T(2,128)(2,1)S(1)} async-done(((bf16[128,2,1440]{2,1,0:T(2,128)(2,1)}), bf16[128,2,1440]{2,1,0:T(2,128)(2,1)S(1)}, u32[]{:S(2)}, u32[]{:S(2)}) %all-to-all-start.1) | async-done | bytes 737312 | tf_op jit(solution)/shard_map/all_to_all | solution.py:52
  194.5 0.6 copy.63
  195.1 0.6 reshape.72
  195.7 0.8 gather_fusion
  196.4 0.1 gather.7
  196.5 1.3 multiply_reduce_fusion
  (11 shorter events, 0.3 us)
Async XLA Ops:
  0.0 1.5 copy-start
  4.5 104.1 %all-to-all-start = ((bf16[128,2,2880]{2,1,0:T(2,128)(2,1)}), bf16[128,2,2880]{2,1,0:T(2,128)(2,1)S(1)}, u32[]{:S(2)}, u32[]{:S(2)}) async-start(bf16[128,2,2880]{2,1,0:T(2,128)(2,1)} %bitcast), calls=%async_computation | async-start | bytes 3014656 | tf_op jit(solution)/shard_map/all_to_all | solution.py:43
  135.0 2.5 %collective-permute-start = (bf16[128,2,1440]{0,2,1:T(8,128)(2,1)S(1)}, bf16[128,2,1440]{0,2,1:T(8,128)(2,1)}, u32[]{:S(2)}, u32[]{:S(2)}) collective-permute-start(bf16[128,2,1440]{0,2,1:T(8,128)(2,1)S(1)} %bitcast.31), channel_id=1, source_target_pairs={{0,1},{1,0},{2,3},{3,2},{4,5},{5,4},{6,7},{7,6},{8,9},{9,8},{10,11... | collective-permute-start | bytes 2211848 | tf_op jit(solution)/shard_map/ppermute | solution.py:10
  138.8 13.9 %copy-start.1 = (s32[16,4]{0,1:T(4,128)S(1)}, s32[16,4]{0,1:T(4,128)}, u32[]{:S(2)}) copy-start(s32[16,4]{0,1:T(4,128)} %param.8) | copy-start | bytes 772
  140.8 53.7 %all-to-all-start.1 = ((bf16[128,2,1440]{2,1,0:T(2,128)(2,1)}), bf16[128,2,1440]{2,1,0:T(2,128)(2,1)S(1)}, u32[]{:S(2)}, u32[]{:S(2)}) async-start(bf16[128,2,1440]{2,1,0:T(2,128)(2,1)} %copy.62), calls=%async_computation.1 | async-start | bytes 1572864 | tf_op jit(solution)/shard_map/all_to_all | solution.py:52
where the time goes:
time: 198 us
  waiting for transfers between devices  114 us (58%)
  starting transfers between devices  44.3 us (22%)
  local copies, waits for them, and re-layouts  23.1 us (12%)
  matrix products  13.4 us (7%)
  other arithmetic  3.09 us (2%)
    all_to_all x1, waiting for transfers between devices, local(): lax.all_to_all(outgoing, 'ep', split_axis=0, concat_axis=0, tiled=True)  71.7 us
    all_to_all x1, waiting for transfers between devices, local(): lax.all_to_all(reduced, 'ep', split_axis=0, concat_axis=0, tiled=True)  41.6 us
    all_to_all x1, starting transfers between devices, local(): lax.all_to_all(outgoing, 'ep', split_axis=0, concat_axis=0, tiled=True)  32.3 us
    all_to_all x1, starting transfers between devices, local(): lax.all_to_all(reduced, 'ep', split_axis=0, concat_axis=0, tiled=True)  11.8 us
    dot_general x1, matrix products, expert_half(): jnp.dot(hidden, w_down, preferred_element_type=jnp.float32)  9.39 us
    dynamic_slice x1, local copies, waits for them, and re-layouts, local(): kept_half = lax.dynamic_index_in_dim(halves, parity, 2, keepdims=False)  4.4 us
    dynamic_slice x1, local copies, waits for them, and re-layouts, local(): given_half = lax.dynamic_index_in_dim(halves, 1 - parity, 2, keepdims=False)  4.08 us
  transfers between devices with their start and end apart: 3, of which 3 were waited for; matrix products, arithmetic and copies ran while one was open for 1% of the time, Pallas kernels for 0%

commit v1 on v0

v1 whole, which is shorter than its diff:
```python
import functools

import jax
import jax.numpy as jnp
from jax import lax
from jax.experimental import pallas as pl
from jax.experimental.pallas import tpu as pltpu
from jax.sharding import PartitionSpec as P

MESH = pl.DeviceIdType.MESH
LANES = 128
CHUNKS = 2
PARTS = 3
BLOCKS = 8


def ring_sizes(mesh):
    row = mesh.devices.reshape(-1, mesh.devices.shape[-1])[0]
    coords = [tuple(d.coords) for d in row]
    cores = coords.count(coords[0])
    across = len({c[0] for c in coords})
    return across, len(row) // (across * cores), cores


def slot_of(way, hop, ring):
    if hop == 0:
        return 0
    if 2 * hop == ring:
        return ring - 1
    return 2 * hop - 1 + way


def kernel(across, ring, tok_hbm, meta_ref, wg_hbm, wu_hbm, wd_hbm, out_ref, tok, gathered, wg, wu, wd,
           select_out, rows_in, part, half_out, half_in, expert_out, returned, combined, sum_in, sum_out,
           load_sem, ag_send, ag_recv, xd_send, xd_recv, fw_send, fw_recv, hp_send, hp_recv,
           xr_send, xr_recv, rs_send, rs_recv):
    count, width = tok.shape
    wide = gathered.shape[2]
    groups = ring // BLOCKS
    held = BLOCKS * count
    reach = ring // 2
    me = lax.axis_index("ep")
    core = lax.rem(me, 2)
    z = lax.rem(me // 2, ring)
    x = me // (2 * ring)

    def at(xx, zz, cc):
        return {"ep": (lax.rem(xx + across, across) * ring + lax.rem(zz + ring, ring)) * 2 + cc}

    ends = (at(x, z + 1, core), at(x, z - 1, core))
    partner = at(x, z, 1 - core)
    sides = [at(x + d, z, core) for d in range(across)]

    tok_load = pltpu.make_async_copy(tok_hbm, tok, load_sem.at[0])
    tok_load.start()
    loads = [pltpu.make_async_copy(s, d, load_sem.at[i + 1])
             for i, (s, d) in enumerate(((wg_hbm, wg), (wu_hbm, wu), (wd_hbm, wd)))]
    barrier = pltpu.get_barrier_semaphore()
    friends = list(ends) + [partner] + sides[1:]
    for friend in friends:
        pl.semaphore_signal(barrier, inc=1, device_id=friend, device_id_type=MESH)
    tok_load.wait()
    gathered[0, :, pl.ds(0, wide - LANES)] = tok[:, pl.ds(0, wide - LANES)]
    tail = width - (wide - LANES)
    gathered[0, :, pl.ds(wide - LANES, tail)] = tok[:, pl.ds(wide - LANES, tail)]
    gathered[0, :, pl.ds(width, LANES - tail)] = meta_ref[:, pl.ds(tail, LANES - tail)]
    pl.semaphore_wait(barrier, len(friends))
    for load in loads:
        load.start()

    edges = [((wide // LANES) * i + CHUNKS - 1) // CHUNKS * LANES for i in range(CHUNKS + 1)]
    spans = [(edges[i], edges[i + 1]) for i in range(CHUNKS)]

    def span(ref, c, full):
        low, high = spans[c]
        return ref.at[:, pl.ds(low, min(high, full) - low)]

    def carries(way, hop, c):
        return hop < reach or (2 * c < CHUNKS) == (way == 0)

    def gather_copy(way, hop, c):
        return pltpu.make_async_remote_copy(
            span(gathered.at[slot_of(way, hop - 1, ring)], c, wide),
            span(gathered.at[slot_of(way, hop, ring)], c, wide),
            ag_send.at[way, hop - 1, c], ag_recv.at[way, hop - 1, c],
            device_id=ends[way], device_id_type=MESH)

    def gather_hop(hop):
        for c in range(CHUNKS):
            for way in range(2):
                if 1 < hop and carries(way, hop - 1, c):
                    gather_copy(way, hop - 1, c).wait_recv()
                if hop <= reach and carries(way, hop, c):
                    gather_copy(way, hop, c).start()

    lane = lax.broadcasted_iota(jnp.int32, (held, LANES), 1)
    token_row = lax.broadcasted_iota(jnp.int32, (held, LANES), 0)
    piece = 2 * BLOCKS
    half_lanes = across * piece
    inner = lax.rem(lane, half_lanes)
    target = lax.rem(inner // piece + x, across)
    wanted = ((target * ring + z) * 2 + lax.rem(inner, 2)).astype(jnp.float32)
    own_block = lax.rem(inner, piece) // 2 == token_row // count
    first_half = lane < half_lanes

    def matches(g):
        meta = gathered[pl.ds(g * BLOCKS, BLOCKS), :, pl.ds(wide - LANES, LANES)]
        return meta.reshape(held, LANES).astype(jnp.float32)

    def choose(g):
        meta = matches(g)
        sel = jnp.zeros((held, LANES), jnp.float32)
        for k in range(4):
            hit = (meta[:, tail + k:tail + k + 1] == wanted) & own_block
            sel = sel + jnp.where(hit, 1.0, 0.0)
        sel_t = sel.T[:half_lanes].astype(jnp.bfloat16)
        data = gathered[pl.ds(g * BLOCKS, BLOCKS), :, pl.ds(0, width)].reshape(held, width)
        picked = jnp.dot(sel_t, data, preferred_element_type=jnp.float32).astype(jnp.bfloat16)
        select_out[g] = picked.reshape(across, piece, width)
        rows_in[g, 0, 0] = picked[:piece]

    def dispatch_copy(g, d):
        return pltpu.make_async_remote_copy(
            select_out.at[g, d], rows_in.at[g, 0, d], xd_send.at[g, d], xd_recv.at[g, d],
            device_id=sides[d], device_id_type=MESH)

    def share_copy(g, d):
        source = select_out.at[g, 0] if d == 0 else rows_in.at[g, 0, d]
        return pltpu.make_async_remote_copy(
            source, rows_in.at[g, 1, d], fw_send.at[g, d], fw_recv.at[g, d],
            device_id=partner, device_id_type=MESH)

    order = [d for d in range(1, across) if d != across // 2] + ([across // 2] if across > 1 else [])

    def dispatch(g):
        choose(g)
        for d in order:
            dispatch_copy(g, d).start()
        share_copy(g, 0).start()

    def share(g):
        for d in order:
            dispatch_copy(g, d).wait_recv()
            share_copy(g, d).start()

    mine = across * piece

    def expert(g):
        for d in [0] + order:
            share_copy(g, d).wait_recv()

        part[g] = jnp.zeros(part.shape[1:], jnp.float32)

        @pl.loop(0, PARTS)
        def _(n):
            data = rows_in[g].reshape(2 * mine, width)
            contract = (((1,), (1,)), ((), ()))
            gate = lax.dot_general(data, wg[n], contract, preferred_element_type=jnp.float32)
            up = lax.dot_general(data, wu[n], contract, preferred_element_type=jnp.float32)
            hidden = (gate / (1.0 + jnp.exp(-gate)) * up).astype(jnp.bfloat16)
            part[g] += jnp.dot(hidden, wd[n], preferred_element_type=jnp.float32)

        half_out[g] = part[g, pl.ds(mine, mine)].astype(jnp.bfloat16)
        half_copy(g).start()

    def half_copy(g):
        return pltpu.make_async_remote_copy(
            half_out.at[g], half_in.at[g], hp_send.at[g], hp_recv.at[g],
            device_id=partner, device_id_type=MESH)

    def return_copy(g, d):
        return pltpu.make_async_remote_copy(
            expert_out.at[g, d], returned.at[g, d], xr_send.at[g, d], xr_recv.at[g, d],
            device_id=sides[(across - d) % across], device_id_type=MESH)

    def give_back(g):
        half_copy(g).wait_recv()
        total = (part[g, pl.ds(0, mine)] + half_in[g].astype(jnp.float32)).astype(jnp.bfloat16)
        expert_out[g] = total.reshape(across, piece, width)
        returned[g, 0] = total[:piece]
        for d in order:
            return_copy(g, d).start()

    def combine(g):
        meta = matches(g)
        mix = jnp.zeros((held, LANES), jnp.float32)
        for k in range(4):
            hit = (meta[:, tail + k:tail + k + 1] == wanted) & own_block
            high = meta[:, tail + 4 + k:tail + 5 + k] / 256.0
            low = meta[:, tail + 8 + k:tail + 9 + k] / 65536.0
            mix = mix + jnp.where(hit, jnp.where(first_half, high, low), 0.0)
        for d in order:
            return_copy(g, d).wait_recv()
        data = returned[g].reshape(mine, width)
        data = jnp.concatenate([data, data], axis=0)
        total = jnp.dot(mix.astype(jnp.bfloat16), data, preferred_element_type=jnp.float32)
        combined[pl.ds(g * BLOCKS, BLOCKS)] = total.reshape(BLOCKS, count, width)

    def sum_copy(way, hop, c):
        return pltpu.make_async_remote_copy(
            span(sum_out.at[way, hop - 1], c, width), span(sum_in.at[way, hop - 1], c, width),
            rs_send.at[way, hop - 1, c], rs_recv.at[way, hop - 1, c],
            device_id=ends[way], device_id_type=MESH)

    def sum_hop(hop):
        for c in range(CHUNKS):
            for way in range(2):
                if not carries(way, hop, c):
                    continue
                low, high = spans[c]
                high = min(high, width)
                value = combined[slot_of(1 - way, hop, ring), :, pl.ds(low, high - low)]
                if hop < reach and carries(way, hop + 1, c):
                    sum_copy(way, hop + 1, c).wait_recv()
                    value = value + sum_in[way, hop, :, pl.ds(low, high - low)].astype(jnp.float32)
                sum_out[way, hop - 1, :, pl.ds(low, high - low)] = value.astype(jnp.bfloat16)
                sum_copy(way, hop, c).start()

    complete = [max(h for h in range(reach + 1) for w in range(2) if slot_of(w, h, ring) < (g + 1) * BLOCKS)
                for g in range(groups)]
    for hop in range(1, reach + 2):
        gather_hop(hop)
        for g in range(groups):
            if complete[g] == hop - 1:
                dispatch(g)
            elif complete[g] == hop - 3:
                share(g)
    for load in loads:
        load.wait()
    for g in range(groups):
        if complete[g] > reach - 2:
            share(g)
        expert(g)
    for g in reversed(range(groups)):
        give_back(g)
    ready = groups
    for hop in range(reach, 0, -1):
        lowest = min(slot_of(w, hop, ring) for w in range(2)) // BLOCKS
        while ready > lowest:
            ready -= 1
            combine(ready)
        sum_hop(hop)
    for c in range(CHUNKS):
        low, high = spans[c]
        high = min(high, width)
        value = combined[0, :, pl.ds(low, high - low)]
        for way in range(2):
            sum_copy(way, 1, c).wait_recv()
            value = value + sum_in[way, 0, :, pl.ds(low, high - low)].astype(jnp.float32)
        out_ref[:, pl.ds(low, high - low)] = value.astype(jnp.bfloat16)

    for hop in range(1, reach + 1):
        for c in range(CHUNKS):
            for way in range(2):
                if carries(way, hop, c):
                    gather_copy(way, hop, c).wait_send()
                    sum_copy(way, hop, c).wait_send()
    for g in range(groups):
        for d in order:
            dispatch_copy(g, d).wait_send()
            return_copy(g, d).wait_send()
        for d in range(across):
            share_copy(g, d).wait_send()
        half_copy(g).wait_send()


def local(across, ring, tokens, routes, gate_fixed, gate_weight, up_weight, down_weight):
    count, width = tokens.shape
    top = routes.shape[1]
    hidden = gate_weight.shape[2]
    wide = -(-width // LANES) * LANES
    tail = width - (wide - LANES)
    earlier = jnp.arange(count)[:, None] > jnp.arange(count)[None, :]
    same = (routes[:, :, None, None] == routes[None, None, :, :]) & earlier[:, None, :, None]
    position = jnp.sum(same.astype(jnp.int32), axis=(2, 3))
    meta = jnp.concatenate([routes * 2 + position, gate_fixed // 256, gate_fixed % 256], axis=1)
    meta = jnp.pad(meta.astype(jnp.bfloat16), ((0, 0), (tail, LANES - tail - 3 * top)))
    groups = ring // BLOCKS
    reach = ring // 2
    piece = 2 * BLOCKS
    mine = across * piece
    held = BLOCKS * count
    bf16, f32 = jnp.bfloat16, jnp.float32
    dma = pltpu.SemaphoreType.DMA
    wg = jnp.swapaxes(gate_weight[0], 0, 1).reshape(PARTS, hidden // PARTS, width)
    wu = jnp.swapaxes(up_weight[0], 0, 1).reshape(PARTS, hidden // PARTS, width)
    wd = down_weight[0].reshape(PARTS, hidden // PARTS, width)
    vmem, anywhere = pl.BlockSpec(memory_space=pltpu.VMEM), pl.BlockSpec(memory_space=pl.ANY)
    return pl.pallas_call(
        functools.partial(kernel, across, ring),
        out_shape=jax.ShapeDtypeStruct((count, width), bf16),
        in_specs=[anywhere, vmem, anywhere, anywhere, anywhere],
        out_specs=vmem,
        scratch_shapes=[
            pltpu.VMEM((count, width), bf16),
            pltpu.VMEM((ring, count, wide), bf16),
            pltpu.VMEM(wg.shape, bf16),
            pltpu.VMEM(wu.shape, bf16),
            pltpu.VMEM(wd.shape, bf16),
            pltpu.VMEM((groups, across, piece, width), bf16),
            pltpu.VMEM((groups, 2, across, piece, width), bf16),
            pltpu.VMEM((groups, 2 * mine, width), f32),
            pltpu.VMEM((groups, mine, width), bf16),
            pltpu.VMEM((groups, mine, width), bf16),
            pltpu.VMEM((groups, across, piece, width), bf16),
            pltpu.VMEM((groups, across, piece, width), bf16),
            pltpu.VMEM((ring, count, width), f32),
            pltpu.VMEM((2, reach, count, width), bf16),
            pltpu.VMEM((2, reach, count, width), bf16),
            dma((4,)),
            dma((2, reach, CHUNKS)), dma((2, reach, CHUNKS)),
            dma((groups, across)), dma((groups, across)),
            dma((groups, across)), dma((groups, across)),
            dma((groups,)), dma((groups,)),
            dma((groups, across)), dma((groups, across)),
            dma((2, reach, CHUNKS)), dma((2, reach, CHUNKS)),
        ],
        compiler_params=pltpu.CompilerParams(
            collective_id=0, has_side_effects=True, vmem_limit_bytes=60 * 1024 * 1024
        ),
    )(tokens, meta, wg, wu, wd)


def solution(mesh):
    across, ring, _ = ring_sizes(mesh)
    placed = (
        P(("groups", "ep"), None),
        P(("groups", "ep"), None),
        P(("groups", "ep"), None),
        P("ep", None, None),
        P("ep", None, None),
        P("ep", None, None),
    )
    return jax.shard_map(
        functools.partial(local, across, ring),
        mesh=mesh, in_specs=placed, out_specs=P(("groups", "ep"), None), check_vma=False,
    )
```

time: 198 us -> 111 us (0.56)
  waiting for transfers between devices: 114 us -> 0 us
  Pallas kernels: 0 us -> 106 us
  starting transfers between devices: 44.3 us -> 0 us
  local copies, waits for them, and re-layouts: 23.1 us -> 3.14 us
  matrix products: 13.4 us -> 0 us
    all_to_all x2 -> x0, waiting for transfers between devices: 113 us -> none  [the longest x1 71.7 us: local(): lax.all_to_all(outgoing, 'ep', split_axis=0, concat_axis=0, tiled=True)]
    pallas_call x0 -> x1, Pallas kernels: none -> 106 us  [local(): pl.pallas_call(functools.partial(kernel, across, ring), out_shape=jax.Sha...]
    all_to_all x2 -> x0, starting transfers between devices: 44.2 us -> none  [the longest x1 32.3 us: local(): lax.all_to_all(outgoing, 'ep', split_axis=0, concat_axis=0, tiled=True)]
    dot_general x3 -> x0, matrix products: 13.4 us -> none  [the longest x1 9.39 us: expert_half(): jnp.dot(hidden, w_down, preferred_element_type=jnp.float32)]
    dynamic_slice x2 -> x0, local copies, waits for them, and re-layouts: 8.48 us -> none  [the longest x1 4.4 us: local(): kept_half = lax.dynamic_index_in_dim(halves, parity, 2, keepdims=False)]
    convert_element_type x3 -> x0, local copies, waits for them, and re-layouts: 4.17 us -> none  [the longest x1 1.98 us: local(): (kept_half.astype(jnp.float32) + partner.astype(jnp.float32)).astype(jnp....]
    broadcast_in_dim x2 -> x0, local copies, waits for them, and re-layouts: 2.22 us -> none  [local(): jnp.broadcast_to(packed, (experts, 2, capacity, width))]
  transfers between devices with their start and end apart: 3 -> 0, of which waited for: 3 -> 0; matrix products, arithmetic and copies ran while one was open for 1% -> 0% of each run, Pallas kernels for 0% -> 0%
where the time goes in v1:
time: 111 us; the launch traced here: 110 us
  Pallas kernels  106 us (95%)
  local copies, waits for them, and re-layouts  3.14 us (3%)
  other arithmetic  1.68 us (2%)
    pallas_call x1, Pallas kernels, local(): pl.pallas_call(functools.partial(kernel, across, ring), out_shape=jax.Sha...  106 us
    unnamed x3, local copies, waits for them, and re-layouts  3.06 us

profile of v1, /device:TPU:40, one launch (start us, length us, event | category | flops | bytes accessed | tf_op | source)
XLA Modules:
  0.0 110.4 jit_solution(16739440046536349532)
XLA Ops:
  0.0 1.0 convert_reduce_fusion
  1.0 0.1 copy.22
  1.1 0.8 copy.23
  1.8 0.8 copy.20
  2.6 0.7 fusion.9.meta_ref
  3.3 105.6 %shard_map.64 = bf16[16,2880]{1,0:T(8,128)(2,1)} custom-call(bf16[16,2880]{1,0:T(8,128)(2,1)} %tok_hbm.1, bf16[16,128]{1,0:T(8,128)(2,1)} %fusion.9.meta_ref, bf16[3,240,2880]{2,1,0:T(8,128)(2,1)} %bitcast.11, bf16[3,240,2880]{2,1,0:T(8,128)(2,1)} %bitcast.12, bf16[3,240,2880]{2,1,0:T(8,128)(2,1)} %bitcast.13), custom_call_target="tpu_custom_call" | custom-call | tf_op jit(solution)/shard_map/pallas_call | solution.py:289
  108.9 1.5 %copy.28 = bf16[16,2880]{1,0:T(8,128)(2,1)} copy(bf16[16,2880]{1,0:T(8,128)(2,1)} %shard_map.64) | data formatting | bytes 184320
  (2 shorter events, 0.0 us)
